TPU v7x, 256 devices: a whole 4x4x8 slice. The times are simulated.
256 devices in a mesh: band: 64 (over x, z_lo, y, core), pw: 4 (over z_hi).
Axes of the slice: x: 4, y: 4, z: 8 (z_hi: 4, z_lo: 2; z = z_hi * 2 + z_lo), core: 2. Of those that a mesh axis runs over, the one named last changes fastest.
Arguments:
- pair_density: bfloat16 [320, 128, 9216], P('band', None, 'pw'), may hold values from -6 to 6
- eigvecs: bfloat16 [2944, 9216], P('band', 'pw'), may hold values from -0.0625 to 0.0625
- screening: bfloat16 [2944, 2944], P('pw'), may hold values from -0.00048828125 to 0.00048828125
- occupation: float32 [128], replicated, may hold values from 0 to 1
- window_start: int32 [320], P('band'), may hold values from 0 to 511, as said below
- window_len: int32 [320], P('band'), may hold values from 1 to 128, as said below
- slot_band: int32 [320], P('band'), may hold values from -1 to 127, as said below
Outputs:
- sigma: float32 [512, 512], P(('band', 'pw'))
Inputs may be any that keep to these rules, and one draw needn't show every extreme that they name: window_start + window_len <= 512 for every slot. `window_len`: some slot has a window of 128 bands. On each index of band the live slots (slot_band >= 0) come first among its 5 slots; each index holds 3 to 5 live slots, and the counts of index i and index i + 64 / 2 add up to 8.
All inputs are finite; a program needn't handle non-finite values.
Results may differ from a plain program's by a relative error of at most 0.0049.
Values may be sent and summed in bfloat16 or wider, within the bound.
A program may use at most 128 MiB of HBM per device.

v0:
```python
import jax
import jax.numpy as jnp
from jax import lax
from jax.sharding import PartitionSpec as P

NB_SIGMA = 512


def from_partner(array, axis, distance):
    return lax.ppermute(array, axis, [(i, i ^ 1 << distance) for i in range(lax.axis_size(axis))])


def in_blocks(array, dim, length):
    lengths = array.shape
    blocks = array.reshape(*lengths[:dim], length, lengths[dim] // length, *lengths[dim + 1 :])
    return jnp.moveaxis(blocks, dim, 0)


def summed_on_arrival(array, axis, dim):
    blocks = in_blocks(array, dim, lax.axis_size(axis))
    arrived = lax.all_to_all(blocks, axis, split_axis=0, concat_axis=0, tiled=True)
    return arrived.astype(jnp.float32).sum(axis=0)


def sum_at_owner(array, axis, dim):
    length = lax.axis_size(axis)
    blocks = lax.all_to_all(in_blocks(array, dim, length), axis, 0, 0, tiled=True)
    return jnp.sum(blocks, axis=0)


def per_device(pair_density, eigvecs, screening, occupation, window_start, window_len, slot_band):
    capacity, block, plane_rows = pair_density.shape
    top_bit = lax.axis_size("band").bit_length() - 2
    live_count = jnp.sum((slot_band >= 0).astype(jnp.int32))
    last = capacity - 1
    spare_meta = jnp.stack([window_start[last], window_len[last], slot_band[last]])
    got_block = from_partner(pair_density[last], "band", top_bit)
    got_meta = from_partner(spare_meta, "band", top_bit)
    taking = live_count == capacity - 2
    kept_density = pair_density[:last]
    density = jnp.where(taking, kept_density.at[last - 1].set(got_block), kept_density)
    starts = jnp.where(
        taking, window_start[:last].at[last - 1].set(got_meta[0]), window_start[:last]
    )
    lengths = jnp.where(taking, window_len[:last].at[last - 1].set(got_meta[1]), window_len[:last])
    band_ids = jnp.where(taking, slot_band[:last].at[last - 1].set(got_meta[2]), slot_band[:last])
    slots = density.shape[0]
    flat = density.reshape(slots * block, plane_rows)
    partial_proj = lax.dot_general(
        flat,
        lax.all_gather(eigvecs, "band", axis=0, tiled=True),
        (((1,), (1,)), ((), ())),
        preferred_element_type=jnp.float32,
    )
    row_ids = jnp.arange(block, dtype=jnp.int32)
    keep_rows = ((row_ids[None, :] < lengths[:, None]) & (band_ids[:, None] >= 0)).astype(
        jnp.float32
    )
    masked = partial_proj * keep_rows.reshape(slots * block, 1)
    share = lax.psum_scatter(masked, "pw", scatter_dimension=1, tiled=True)
    projected = lax.all_gather(share.astype(jnp.bfloat16), "pw", axis=1, tiled=True)
    width = screening.shape[0]
    own_cols = lax.dynamic_slice_in_dim(projected, lax.axis_index("pw") * width, width, 1)
    screened = lax.dot_general(
        projected, screening, (((1,), (1,)), ((), ())), preferred_element_type=jnp.float32
    ).astype(jnp.bfloat16)
    block_sigma = lax.dot_general(
        screened.reshape(slots, block, width),
        own_cols.reshape(slots, block, width),
        (((2,), (2,)), ((0,), (0,))),
        preferred_element_type=jnp.float32,
    )
    band_list = jnp.arange(occupation.shape[0], dtype=jnp.int32)
    weights = 0.5 - jnp.sum(
        jnp.where(band_list[None, :] == band_ids[:, None], occupation[None, :], 0.0), axis=1
    )
    totals = jnp.zeros((NB_SIGMA + block, NB_SIGMA + block), jnp.float32)
    for index in range(slots):
        first = starts[index]
        previous = lax.dynamic_slice(totals, (first, first), (block, block))
        totals = lax.dynamic_update_slice(
            totals, previous + weights[index] * block_sigma[index], (first, first)
        )
    sigma_part = totals[:NB_SIGMA, :NB_SIGMA]
    by_band = summed_on_arrival(sigma_part.astype(jnp.bfloat16), "band", 0)
    return sum_at_owner(by_band, "pw", 0)


def solution(mesh):
    return jax.shard_map(
        per_device,
        mesh=mesh,
        in_specs=(
            P("band", None, "pw"),
            P("band", "pw"),
            P("pw", None),
            P(),
            P("band"),
            P("band"),
            P("band"),
        ),
        out_specs=P(("band", "pw"), None),
        check_vma=False,
    )
```

profile of v0, /device:TPU:1, one launch (start us, length us, event | category | flops | bytes accessed | tf_op | source)
XLA Modules:
  0.0 408.9 jit_solution(6931820106926020516)
XLA Ops:
  6.5 0.7 all-gather.6.cloned.1.call-update
  7.3 1.3 slice.139
  8.6 1.5 fusion.16
  10.1 2.0 pad_add_fusion
  12.1 3.6 collective-permute-start
  15.7 1.1 slice_bitcast_fusion
  17.1 1.2 slice_bitcast_fusion.1
  18.3 1.3 fusion.14
  20.3 0.7 fusion.17
  22.2 1.2 select_n.61
  23.5 0.6 compare_bitcast_fusion
  24.2 12.2 %collective-permute-done.1 = bf16[128,2304]{1,0:T(8,128)(2,1)S(1)} collective-permute-done((bf16[128,2304]{1,0:T(8,128)(2,1)S(1)}, bf16[128,2304]{1,0:T(8,128)(2,1)S(1)}, u32[]{:S(2)}, u32[]{:S(2)}) %collective-permute-start.1) | collective-permute-done | bytes 589856 | tf_op jit(solution)/shard_map/ppermute | solution.py:10
  36.3 1.2 fusion.4
  37.5 103.1 %all-gather.6.cloned.1.call-done = bf16[64,46,2304]{2,1,0:T(8,128)(2,1)} async-done(((bf16[1,46,2304]{2,1,0:T(8,128)(2,1)}), bf16[64,46,2304]{2,1,0:T(8,128)(2,1)}) %all-gather.6.cloned.1.call-update) | async-done | bytes 13565968 | tf_op jit(solution)/shard_map/all_gather | solution.py:51
  140.7 16.9 %reshape.157 = bf16[2944,2304]{1,0:T(8,128)(2,1)} reshape(bf16[64,46,2304]{2,1,0:T(8,128)(2,1)} %all-gather.6.cloned.1.call-done) | data formatting | bytes 27131904
  157.6 12.1 %convolution_multiply_fusion = f32[512,2944]{0,1:T(8,128)} fusion(bf16[512,2304]{1,0:T(8,128)(2,1)S(1)} %bitcast.53, bf16[2944,2304]{1,0:T(8,128)(2,1)} %reshape.157, f32[512]{0:T(512)S(1)} %convert_bitcast_fusion), kind=kOutput, calls=%fused_computation | convolution fusion | flops 6947274752 | bytes 21956608 | tf_op jit(solution)/shard_map/dot_general | solution.py:49
  169.8 115.1 %reduce-scatter.2.cloned.1.call-done = f32[512,736]{0,1:T(8,128)} async-done(((f32[512,2944]{0,1:T(8,128)}), f32[512,736]{0,1:T(8,128)}) %reduce-scatter.2.cloned.1.call-update) | async-done | bytes 1507344 | tf_op jit(solution)/shard_map/reduce_scatter | solution.py:60
  284.9 2.4 convert_element_type.26
  294.4 0.6 fusion.15
  295.0 51.6 %all-gather.4.cloned.1.call-done = bf16[512,2944]{0,1:T(8,128)(2,1)} async-done(((bf16[512,736]{0,1:T(8,128)(2,1)}), bf16[512,2944]{0,1:T(8,128)(2,1)}) %all-gather.4.cloned.1.call-update) | async-done | bytes 3014672 | tf_op jit(solution)/shard_map/all_gather | solution.py:61
  346.6 1.2 constant_dynamic-slice_fusion
  348.1 5.7 %fusion = bf16[92,4,8,128]{3,2,1,0:T(8,128)(2,1)S(1)} fusion(bf16[736,2944]{1,0:T(8,128)(2,1)} %param.17, bf16[512,2944]{0,1:T(8,128)(2,1)} %all-gather.4.cloned.1.call-done), kind=kOutput, calls=%fused_computation.2 | convolution fusion | flops 2219163648 | bytes 8101888 | tf_op jit(solution)/shard_map/dot_general | solution.py:64
  354.8 2.1 dynamic_update_slice.12
  356.9 0.7 fusion.11
  357.6 2.1 dynamic_update_slice.13
  359.7 0.7 fusion.9
  360.4 2.1 dynamic_update_slice.14
  362.5 0.7 fusion.7
  363.2 2.1 dynamic_update_slice.15
  365.4 26.5 %all_to_all.10 = bf16[64,8,512]{2,1,0:T(8,128)(2,1)S(1)} all-to-all(bf16[64,8,512]{2,1,0:T(8,128)(2,1)S(1)} %fusion.5), channel_id=1, replica_groups=mesh['band'=64,'pw'=4] {'band'}, dimensions={0} | all-to-all | bytes 1048576 | tf_op jit(solution)/shard_map/all_to_all | solution.py:21
  392.0 9.7 %all_to_all.11 = f32[4,2,512]{2,1,0:T(2,128)S(1)} all-to-all(f32[4,2,512]{2,1,0:T(2,128)S(1)} %reshape.154), channel_id=1, replica_groups=mesh['band'=64,'pw'=4] {'pw'}, dimensions={0} | all-to-all | bytes 32768 | tf_op jit(solution)/shard_map/all_to_all | solution.py:27
  401.8 0.6 reduce_sum.39
  (26 shorter events, 2.2 us)
Async XLA Ops:
  6.5 134.1 %all-gather.6.cloned.1.call-start = ((), (), s32[]{:S(2)}) async-start(), calls=%async_computation.5 | async-start | bytes 14376960 | tf_op jit(solution)/shard_map/all_gather | solution.py:51
  7.3 277.6 %reduce-scatter.2.cloned.1.call-start = ((), (), s32[]{:S(2)}) async-start(), calls=%async_computation.3 | async-start | bytes 7536640 | tf_op jit(solution)/shard_map/reduce_scatter | solution.py:60
  12.1 7.5 %copy-start = (s32[5]{0:T(128)S(1)}, s32[5]{0:T(128)}, u32[]{:S(2)}) copy-start(s32[5]{0:T(128)} %param.20) | copy-start | bytes 64
  12.1 24.2 %slice-start = ((bf16[5,128,2304]{2,1,0:T(8,128)(2,1)}), bf16[4,128,2304]{2,1,0:T(8,128)(2,1)S(1)}, s32[]{:S(2)}) async-start(bf16[5,128,2304]{2,1,0:T(8,128)(2,1)} %param.15), calls=%async_computation.6 | async-start | bytes 4718592 | tf_op jit(solution)/shard_map/slice | solution.py:40
  12.1 8.1 %collective-permute-start = (s32[3]{0:T(128)S(1)}, s32[3]{0:T(128)S(1)}, u32[]{:S(2)}, u32[]{:S(2)}) collective-permute-start(s32[3]{0:T(128)S(1)} %pad_add_fusion), channel_id=1, source_target_pairs={{0,128},{4,132},{8,136},{12,140},{16,144},{20,148},{24,152},{28,15... | collective-permute-start | bytes 44 | tf_op jit(solution)/shard_map/ppermute | solution.py:10
  16.9 19.5 %collective-permute-start.1 = (bf16[128,2304]{1,0:T(8,128)(2,1)S(1)}, bf16[128,2304]{1,0:T(8,128)(2,1)S(1)}, u32[]{:S(2)}, u32[]{:S(2)}) collective-permute-start(bf16[128,2304]{1,0:T(8,128)(2,1)S(1)} %slice_bitcast_fusion), channel_id=1, source_target_pairs={{0,128},{4,132},{8,136},{12,140},{16,144},{20,148},{24,152},{28,15... | collective-permute-start | bytes 1769480 | tf_op jit(solution)/shard_map/ppermute | solution.py:10
  169.7 124.5 %copy-start.1 = (f32[128]{0:T(128)S(1)}, f32[128]{0:T(128)}, u32[]{:S(2)}) copy-start(f32[128]{0:T(128)} %param.18) | copy-start | bytes 1540
  169.7 124.5 %copy-start.2 = (s32[4,1]{0,1:T(1,128)S(1)}, s32[4,1]{0,1:T(1,128)}, u32[]{:S(2)}) copy-start(s32[4,1]{0,1:T(1,128)} %select_n.61) | copy-start | bytes 52
  169.7 176.9 %all-gather.4.cloned.1.call-start = ((), (), s32[]{:S(2)}) async-start(), calls=%async_computation.4 | async-start | bytes 3768320 | tf_op jit(solution)/shard_map/all_gather | solution.py:61
Sparse Core Ops, SparseCore 0:
  9.2 131.4 all-gather.5
  169.8 115.0 reduce-scatter.1
  287.4 59.1 all-gather.3
where the time goes:
time: 410 us; the launch traced here: 409 us
  waiting for transfers between devices  283 us (69%)
  blocking collectives  36.3 us (9%)
  local copies, waits for them, and re-layouts  33.8 us (8%)
  between operations  22.1 us (5%)
  matrix products  18.1 us (4%)
  other arithmetic  11.9 us (3%)
    reduce_scatter x1, waiting for transfers between devices, per_device(): share = lax.psum_scatter(masked, 'pw', scatter_dimension=1, tiled=True)  115 us
    all_gather x1, waiting for transfers between devices, per_device(): lax.all_gather(eigvecs, 'band', axis=0, tiled=True)  103 us
    all_gather x1, waiting for transfers between devices, per_device(): lax.all_gather(share.astype(jnp.bfloat16), 'pw', axis=1, tiled=True)  51.6 us
    all_to_all x1, blocking collectives, summed_on_arrival(): lax.all_to_all(blocks, axis, split_axis=0, concat_axis=0, tiled=True)  26.5 us
    unnamed x8, local copies, waits for them, and re-layouts  17 us
    ppermute x2, waiting for transfers between devices, from_partner(): lax.ppermute(array, axis, [(i, i ^ 1 << distance) for i in range(lax.axis...  12.2 us
    dot_general x1, matrix products, per_device(): lax.dot_general(flat, lax.all_gather(eigvecs, 'band', axis=0, tiled=True)...  12.1 us
    all_to_all x1, blocking collectives, sum_at_owner(): lax.all_to_all(in_blocks(array, dim, length), axis, 0, 0, tiled=True)  9.74 us
  transfers between devices with their start and end apart: 5, of which 4 were waited for; matrix products, arithmetic and copies ran while one was open for 3% of the time, Pallas kernels for 0%

commit v1 on v0

--- a/solution.py
+++ b/solution.py
@@ -48,7 +48,9 @@
     flat = density.reshape(slots * block, plane_rows)
     partial_proj = lax.dot_general(
         flat,
-        lax.all_gather(eigvecs, "band", axis=0, tiled=True),
+        jnp.concatenate(
+            lax.all_to_all(jnp.stack([eigvecs] * lax.axis_size("band")), "band", 0, 0), axis=0
+        ),
         (((1,), (1,)), ((), ())),
         preferred_element_type=jnp.float32,
     )

time: 410 us -> 497 us (1.21)
  waiting for transfers between devices: 283 us -> 353 us
  starting transfers between devices: 3.95 us -> 14 us
  local copies, waits for them, and re-layouts: 33.8 us -> 39.5 us
    ppermute x2, waiting for transfers between devices: 12.2 us -> 167 us  [from_partner(): lax.ppermute(array, axis, [(i, i ^ 1 << distance) for i in range(lax.axis...]
    all_gather x1 -> x0, waiting for transfers between devices: 103 us -> none  [per_device(): lax.all_gather(eigvecs, 'band', axis=0, tiled=True)]
    reshape x0 -> x1, local copies, waits for them, and re-layouts: none -> 17 us  [per_device(): jnp.concatenate(lax.all_to_all(jnp.stack([eigvecs] * lax.axis_size('band'...]
    unnamed x8 -> x15, local copies, waits for them, and re-layouts: 17 us -> 0.03 us
    reduce_scatter x1, waiting for transfers between devices: 115 us -> 128 us  [per_device(): share = lax.psum_scatter(masked, 'pw', scatter_dimension=1, tiled=True)]
    all_to_all x0 -> x1, starting transfers between devices: none -> 10.8 us  [per_device(): lax.all_to_all(jnp.stack([eigvecs] * lax.axis_size('band')), 'band', 0, 0)]
    all_to_all x0 -> x1, waiting for transfers between devices: none -> 7.53 us  [per_device(): lax.all_to_all(jnp.stack([eigvecs] * lax.axis_size('band')), 'band', 0, 0)]
    another operation x1 -> x2, local copies, waits for them, and re-layouts: 1.5 us -> 7.64 us  [the longest x1 6.97 us: per_device(): jnp.stack([eigvecs] * lax.axis_size('band'))]
  transfers between devices with their start and end apart: 5 -> 5, of which waited for: 4 -> 5; matrix products, arithmetic and copies ran while one was open for 3% -> 2% of each run, Pallas kernels for 0% -> 0%
where the time goes in v1:
time: 497 us; the launch traced here: 496 us
  waiting for transfers between devices  353 us (71%)
  local copies, waits for them, and re-layouts  39.5 us (8%)
  blocking collectives  36.3 us (7%)
  between operations  22.6 us (5%)
  matrix products  18.1 us (4%)
  starting transfers between devices  14 us (3%)
  other arithmetic  12.1 us (2%)
    ppermute x2, waiting for transfers between devices, from_partner(): lax.ppermute(array, axis, [(i, i ^ 1 << distance) for i in range(lax.axis...  167 us
    reduce_scatter x1, waiting for transfers between devices, per_device(): share = lax.psum_scatter(masked, 'pw', scatter_dimension=1, tiled=True)  128 us
    all_gather x1, waiting for transfers between devices, per_device(): lax.all_gather(share.astype(jnp.bfloat16), 'pw', axis=1, tiled=True)  51.3 us
    all_to_all x1, blocking collectives, summed_on_arrival(): lax.all_to_all(blocks, axis, split_axis=0, concat_axis=0, tiled=True)  26.5 us
    reshape x1, local copies, waits for them, and re-layouts, per_device(): jnp.concatenate(lax.all_to_all(jnp.stack([eigvecs] * lax.axis_size('band'...  17 us
    dot_general x1, matrix products, per_device(): lax.dot_general(flat, jnp.concatenate(lax.all_to_all(jnp.stack([eigvecs]...  12 us
    all_to_all x1, starting transfers between devices, per_device(): lax.all_to_all(jnp.stack([eigvecs] * lax.axis_size('band')), 'band', 0, 0)  10.8 us
  transfers between devices with their start and end apart: 5, of which 5 were waited for; matrix products, arithmetic and copies ran while one was open for 2% of the time, Pallas kernels for 0%

profile of v1, /device:TPU:1, one launch (start us, length us, event | category | flops | bytes accessed | tf_op | source)
XLA Modules:
  0.0 496.0 jit_solution(769066479059651475)
XLA Ops:
  6.5 7.0 %stack.5 = bf16[64,46,2304]{2,1,0:T(8,128)(2,1)} broadcast(bf16[46,2304]{1,0:T(8,128)(2,1)} %param.16), dimensions={1,2} | broadcast | bytes 13777920 | tf_op jit(solution)/shard_map/stack | solution.py:52
  13.5 10.8 %all-to-all-start = ((bf16[64,46,2304]{2,1,0:T(8,128)(2,1)}), bf16[64,46,2304]{2,1,0:T(8,128)(2,1)}, u32[]{:S(2)}, u32[]{:S(2)}) async-start(bf16[64,46,2304]{2,1,0:T(8,128)(2,1)} %stack.5), calls=%async_computation | async-start | bytes 28311552 | tf_op jit(solution)/shard_map/all_to_all | solution.py:52
  25.0 0.7 fusion.16
  25.6 2.0 pad_add_fusion
  27.6 3.0 collective-permute-start
  31.4 0.6 fusion.14
  32.0 1.7 slice.144
  34.3 153.1 %collective-permute-done = s32[3]{0:T(128)S(1)} collective-permute-done((s32[3]{0:T(128)S(1)}, s32[3]{0:T(128)S(1)}, u32[]{:S(2)}, u32[]{:S(2)}) %collective-permute-start) | collective-permute-done | bytes 44 | tf_op jit(solution)/shard_map/ppermute | solution.py:10
  187.4 0.7 fusion.17
  189.4 1.4 select_n.61
  190.8 0.7 compare_bitcast_fusion
  191.6 13.9 %collective-permute-done.1 = bf16[128,2304]{1,0:T(8,128)(2,1)} collective-permute-done((bf16[128,2304]{1,0:T(8,128)(2,1)S(1)}, bf16[128,2304]{1,0:T(8,128)(2,1)}, u32[]{:S(2)}, u32[]{:S(2)}) %collective-permute-start.1) | collective-permute-done | bytes 589856 | tf_op jit(solution)/shard_map/ppermute | solution.py:10
  205.5 2.0 fusion.4
  207.5 7.5 %all-to-all-done = bf16[64,46,2304]{2,1,0:T(8,128)(2,1)} async-done(((bf16[64,46,2304]{2,1,0:T(8,128)(2,1)}), bf16[64,46,2304]{2,1,0:T(8,128)(2,1)}, u32[]{:S(2)}, u32[]{:S(2)}) %all-to-all-start) | async-done | bytes 13565984 | tf_op jit(solution)/shard_map/all_to_all | solution.py:52
  215.1 17.0 %reshape.156 = bf16[2944,2304]{1,0:T(8,128)(2,1)} reshape(bf16[64,46,2304]{2,1,0:T(8,128)(2,1)} %all-to-all-done) | data formatting | bytes 27131904 | tf_op jit(solution)/shard_map/reshape | solution.py:51
  232.0 12.0 %convolution_multiply_fusion = f32[512,2944]{0,1:T(8,128)} fusion(bf16[512,2304]{1,0:T(8,128)(2,1)S(1)} %bitcast.53, bf16[2944,2304]{1,0:T(8,128)(2,1)} %reshape.156, f32[512]{0:T(512)S(1)} %convert_bitcast_fusion), kind=kOutput, calls=%fused_computation | convolution fusion | flops 6947274752 | bytes 21956608 | tf_op jit(solution)/shard_map/dot_general | solution.py:49
  244.2 127.6 %reduce-scatter.2.cloned.1.call-done = f32[512,736]{0,1:T(8,128)} async-done(((f32[512,2944]{0,1:T(8,128)}), f32[512,736]{0,1:T(8,128)}) %reduce-scatter.2.cloned.1.call-update) | async-done | bytes 1507344 | tf_op jit(solution)/shard_map/reduce_scatter | solution.py:62
  371.8 2.4 convert_element_type.26
  381.4 0.6 fusion.15
  382.0 51.3 %all-gather.2.cloned.1.call-done = bf16[512,2944]{0,1:T(8,128)(2,1)} async-done(((bf16[512,736]{0,1:T(8,128)(2,1)}), bf16[512,2944]{0,1:T(8,128)(2,1)}) %all-gather.2.cloned.1.call-update) | async-done | bytes 3014672 | tf_op jit(solution)/shard_map/all_gather | solution.py:63
  433.3 1.2 constant_dynamic-slice_fusion
  434.8 5.7 %fusion = bf16[92,4,8,128]{3,2,1,0:T(8,128)(2,1)S(1)} fusion(bf16[736,2944]{1,0:T(8,128)(2,1)} %param.17, bf16[512,2944]{0,1:T(8,128)(2,1)} %all-gather.2.cloned.1.call-done), kind=kOutput, calls=%fused_computation.2 | convolution fusion | flops 2219163648 | bytes 8101888 | tf_op jit(solution)/shard_map/dot_general | solution.py:66
  440.9 0.6 fusion.12
  441.6 2.1 dynamic_update_slice.12
  443.7 0.6 fusion.11
  444.3 2.1 dynamic_update_slice.13
  446.4 0.7 fusion.9
  447.2 2.1 dynamic_update_slice.14
  449.2 0.7 fusion.7
  450.0 2.1 dynamic_update_slice.15
  452.1 26.5 %all_to_all.15 = bf16[64,8,512]{2,1,0:T(8,128)(2,1)S(1)} all-to-all(bf16[64,8,512]{2,1,0:T(8,128)(2,1)S(1)} %fusion.5), channel_id=1, replica_groups=mesh['band'=64,'pw'=4] {'band'}, dimensions={0} | all-to-all | bytes 1048576 | tf_op jit(solution)/shard_map/all_to_all | solution.py:21
  478.8 9.7 %all_to_all.16 = f32[4,2,512]{2,1,0:T(2,128)S(1)} all-to-all(f32[4,2,512]{2,1,0:T(2,128)S(1)} %reshape.160), channel_id=1, replica_groups=mesh['band'=64,'pw'=4] {'pw'}, dimensions={0} | all-to-all | bytes 32768 | tf_op jit(solution)/shard_map/all_to_all | solution.py:27
  (33 shorter events, 3.3 us)
Async XLA Ops:
  13.5 10.8 %copy-start.4 = (s32[5]{0:T(128)S(1)}, s32[5]{0:T(128)}, u32[]{:S(2)}) copy-start(s32[5]{0:T(128)} %param.20) | copy-start | bytes 64
  13.5 11.5 %copy-start.2 = (s32[5]{0:T(128)S(1)}, s32[5]{0:T(128)}, u32[]{:S(2)}) copy-start(s32[5]{0:T(128)} %param.19) | copy-start | bytes 64
  13.5 11.5 %copy-start.3 = (s32[5]{0:T(128)S(1)}, s32[5]{0:T(128)}, u32[]{:S(2)}) copy-start(s32[5]{0:T(128)} %param.21) | copy-start | bytes 64
  13.5 17.1 %copy-start = (bf16[5,128,2304]{2,1,0:T(8,128)(2,1)S(1)}, bf16[5,128,2304]{2,1,0:T(8,128)(2,1)}, u32[]{:S(2)}) copy-start(bf16[5,128,2304]{2,1,0:T(8,128)(2,1)} %param.15) | copy-start | bytes 8847364
  13.5 201.6 %all-to-all-start = ((bf16[64,46,2304]{2,1,0:T(8,128)(2,1)}), bf16[64,46,2304]{2,1,0:T(8,128)(2,1)}, u32[]{:S(2)}, u32[]{:S(2)}) async-start(bf16[64,46,2304]{2,1,0:T(8,128)(2,1)} %stack.5), calls=%async_computation | async-start | bytes 28311552 | tf_op jit(solution)/shard_map/all_to_all | solution.py:52
  24.3 347.5 %reduce-scatter.2.cloned.1.call-start = ((), (), s32[]{:S(2)}) async-start(), calls=%async_computation.4 | async-start | bytes 7536640 | tf_op jit(solution)/shard_map/reduce_scatter | solution.py:62
  27.6 159.8 %collective-permute-start = (s32[3]{0:T(128)S(1)}, s32[3]{0:T(128)S(1)}, u32[]{:S(2)}, u32[]{:S(2)}) collective-permute-start(s32[3]{0:T(128)S(1)} %pad_add_fusion), channel_id=1, source_target_pairs={{0,128},{4,132},{8,136},{12,140},{16,144},{20,148},{24,152},{28,15... | collective-permute-start | bytes 44 | tf_op jit(solution)/shard_map/ppermute | solution.py:10
  30.7 174.8 %collective-permute-start.1 = (bf16[128,2304]{1,0:T(8,128)(2,1)S(1)}, bf16[128,2304]{1,0:T(8,128)(2,1)}, u32[]{:S(2)}, u32[]{:S(2)}) collective-permute-start(bf16[128,2304]{1,0:T(8,128)(2,1)S(1)} %slice_bitcast_fusion), channel_id=1, source_target_pairs={{0,128},{4,132},{8,136},{12,140},{16,144},{20,148},{24,152},{28,15... | collective-permute-start | bytes 1769480 | tf_op jit(solution)/shard_map/ppermute | solution.py:10
  207.5 24.5 %copy-start.1 = (bf16[4,128,2304]{2,1,0:T(8,128)(2,1)S(1)}, bf16[4,128,2304]{2,1,0:T(8,128)(2,1)}, u32[]{:S(2)}) copy-start(bf16[4,128,2304]{2,1,0:T(8,128)(2,1)} %fusion.4) | copy-start | bytes 7077892
  244.1 137.1 %copy-start.5 = (f32[128]{0:T(128)S(1)}, f32[128]{0:T(128)}, u32[]{:S(2)}) copy-start(f32[128]{0:T(128)} %param.18) | copy-start | bytes 1540
  244.1 137.1 %copy-start.6 = (s32[4,1]{0,1:T(1,128)S(1)}, s32[4,1]{0,1:T(1,128)}, u32[]{:S(2)}) copy-start(s32[4,1]{0,1:T(1,128)} %select_n.61) | copy-start | bytes 52
  244.1 189.2 %all-gather.2.cloned.1.call-start = ((), (), s32[]{:S(2)}) async-start(), calls=%async_computation.5 | async-start | bytes 3768320 | tf_op jit(solution)/shard_map/all_gather | solution.py:63
Sparse Core Ops, SparseCore 0:
  244.2 127.4 reduce-scatter.1
  374.3 59.0 all-gather.1
